TPU v7x, 32 devices: a whole 2x2x4 slice. The times are simulated.
32 devices in a mesh: pb: 4 (over x, core), dev: 8 (over z, y).
Axes of the slice: x: 2, y: 2, z: 4, core: 2. Of those that a mesh axis runs over, the one named last changes fastest.
Arguments:
- queries: bfloat16 [64, 768], P(('pb', 'dev')), may hold values from -6 to 6
- probes: int32 [64, 16], P(('pb', 'dev')), may hold values from 0 to 1023, all different within a row
- vectors: bfloat16 [16384, 768], P(('pb', 'dev')), may hold values from -0.4375 to 0.4375
- list_ids: int32 [16384], P(('pb', 'dev')), may hold values from 0 to 1023, as said below
Outputs:
- leaders: float32 [64, 100], P(('pb', 'dev'))
Inputs may be any that keep to these rules, and one draw needn't show every extreme that they name: `list_ids`: each list id names exactly 16 database vectors. `probes`: each query names 16 different lists.
All inputs are finite; a program needn't handle non-finite values.
Results may differ from a plain program's by a relative error of at most 0.0004.
Values may be sent and summed in bfloat16 or wider, within the bound.
A program may use at most 64 MiB of HBM per device.

v0:
```python
import math
import jax
import jax.numpy as jnp
from jax import lax
from jax.sharding import PartitionSpec as P

K = 100
NLIST = 1024
masked_value = -1e30


def filtered_scores(block_rows, block_probes, slab_part, list_onehot):
    products = lax.dot_general(
        block_rows, slab_part, (((1,), (1,)), ((), ())), preferred_element_type=jnp.float32
    )
    count = block_rows.shape[0]
    row_index = lax.broadcasted_iota(jnp.int32, block_probes.shape, 0)
    hits = (
        jnp.zeros((count, list_onehot.shape[0]), jnp.bfloat16)
        .at[row_index, block_probes]
        .set(jnp.bfloat16(1.0))
    )
    matches = jnp.dot(hits, list_onehot, preferred_element_type=jnp.float32)
    return jnp.where(matches > 0.5, products, jnp.float32(masked_value))


def local(queries, probes, vectors, list_ids):
    local_count = min(K, vectors.shape[0])
    list_index = lax.broadcasted_iota(jnp.int32, (NLIST, list_ids.shape[0]), 0)
    list_onehot = (list_index == list_ids[None, :]).astype(jnp.bfloat16)
    block_rows, block_probes = lax.all_gather((queries, probes), ("pb", "dev"), axis=0, tiled=True)
    count = block_rows.shape[0]
    width = math.gcd(count, 256)

    def one_block(block_args):
        rows_here, probes_here = block_args
        kept, _ = lax.top_k(
            filtered_scores(rows_here, probes_here, vectors, list_onehot), local_count
        )
        return kept

    kept = lax.map(
        one_block,
        (
            block_rows.reshape(count // width, width, block_rows.shape[1]),
            block_probes.reshape(count // width, width, block_probes.shape[1]),
        ),
    )
    candidates = kept.reshape(count, local_count)
    pooled = lax.all_to_all(
        lax.all_to_all(candidates, "pb", split_axis=0, concat_axis=1, tiled=True),
        "dev",
        split_axis=0,
        concat_axis=1,
        tiled=True,
    )
    leaders, _ = lax.top_k(pooled, K)
    return leaders


def solution(mesh):
    return jax.shard_map(
        local,
        mesh=mesh,
        in_specs=(
            P(("pb", "dev"), None),
            P(("pb", "dev"), None),
            P(("pb", "dev"), None),
            P(("pb", "dev")),
        ),
        out_specs=P(("pb", "dev"), None),
        check_vma=False,
    )
```

profile of v0, /device:TPU:0, one launch (start us, length us, event | category | flops | bytes accessed | tf_op | source)
XLA Modules:
  0.0 173.4 jit_solution(18283265919945762596)
XLA Ops:
  0.0 0.0 copy-start
  0.0 0.0 copy-start.1
  0.0 70.2 %all-gather = s32[32,2,16]{2,1,0:T(2,128)S(1)} all-gather(s32[1,2,16]{2,1,0:T(2,128)} %bitcast.16), channel_id=1, replica_groups=mesh['pb'=4,'dev'=8] {'pb','dev'}, dimensions={0}, use_global_device_ids=true | all-gather | bytes 4224 | tf_op jit(solution)/shard_map/all_gather | solution.py:31
  70.2 0.1 copy.13
  70.3 0.7 multiply_reduce_fusion
  71.0 0.7 and_reduce_fusion
  71.8 0.1 copy.16
  71.9 0.1 reshape.32
  71.9 7.7 %scatter_custom_fusion = bf16[65536]{0:T(1024)(128)(2,1)S(1)} fusion(s32[1024]{0:T(1024)S(1)} %reshape.32, bf16[1024]{0:T(1024)(128)(2,1)S(1)} %broadcast.64, bf16[]{:T(256)} %constant.41.clone.1), kind=kCustom, calls=%fused_computation.6 | custom fusion | bytes 131074
  79.6 0.1 reshape.31
  79.7 64.1 %all-gather.1 = bf16[32,2,768]{2,1,0:T(2,128)(2,1)S(1)} all-gather(bf16[1,2,768]{2,1,0:T(2,128)(2,1)} %bitcast.15), channel_id=1, replica_groups=mesh['pb'=4,'dev'=8] {'pb','dev'}, dimensions={0}, use_global_device_ids=true | all-gather | bytes 101376 | tf_op jit(solution)/shard_map/all_gather | solution.py:31
  143.8 0.0 copy-done.1
  143.8 0.5 fusion.1
  144.3 0.0 copy-done
  144.3 0.4 convolution_select_fusion
  144.7 3.2 %sort_prefixfusion = f32[64,100]{1,0:T(8,128)S(1)} fusion(f32[64,512]{1,0:T(8,128)S(1)} %convolution_select_fusion), kind=kCustom, calls=%top_k.14.sort_prefix | custom fusion | flops 491520 | bytes 156672 | tf_op jit(solution)/shard_map/while/body/eval_jaxpr/top_k | solution.py:37
  147.9 6.3 %all_to_all.35 = f32[4,16,100]{2,1,0:T(8,128)S(1)} all-to-all(f32[4,16,100]{2,1,0:T(8,128)S(1)} %bitcast.11), channel_id=1, replica_groups=mesh['pb'=4,'dev'=8] {'pb'}, dimensions={0} | all-to-all | bytes 51200 | tf_op jit(solution)/shard_map/all_to_all | solution.py:51
  154.2 0.1 all_to_all.29
  154.3 10.0 %all_to_all.36 = f32[8,2,400]{2,1,0:T(2,128)S(1)} all-to-all(f32[8,2,400]{2,1,0:T(2,128)S(1)} %all_to_all.29), channel_id=1, replica_groups=mesh['pb'=4,'dev'=8] {'dev'}, dimensions={0} | all-to-all | bytes 51200 | tf_op jit(solution)/shard_map/all_to_all | solution.py:50
  164.3 0.1 all_to_all.32
  164.4 8.4 %top_k.20 = (f32[2,3200]{1,0:T(2,128)S(1)}, s32[2,3200]{1,0:T(2,128)}) sort(f32[2,3200]{1,0:T(2,128)S(1)} %all_to_all.32, s32[2,3200]{1,0:T(2,128)S(1)} %iota.24), dimensions={1}, to_apply=%region_2.3 | sort | flops 83200 | bytes 102400 | tf_op jit(solution)/shard_map/top_k | solution.py:57
  172.8 0.6 top_k.21
  (8 shorter events, 0.1 us)
Async XLA Ops:
  0.0 144.3 %copy-start = (bf16[512,768]{1,0:T(8,128)(2,1)S(1)}, bf16[512,768]{1,0:T(8,128)(2,1)}, u32[]{:S(2)}) copy-start(bf16[512,768]{1,0:T(8,128)(2,1)} %param.6) | copy-start | bytes 2359300
  0.0 143.8 %copy-start.1 = (s32[512]{0:T(512)S(1)}, s32[512]{0:T(512)}, u32[]{:S(2)}) copy-start(s32[512]{0:T(512)} %param.7) | copy-start | bytes 6148
where the time goes:
time: 174 us; the launch traced here: 173 us
  blocking collectives  151 us (87%)
  other arithmetic  13.1 us (8%)
  local copies, waits for them, and re-layouts  8.8 us (5%)
    all_gather x2, blocking collectives, local(): lax.all_gather((queries, probes), ('pb', 'dev'), axis=0, tiled=True)  134 us
    all_to_all x1, blocking collectives, local(): lax.all_to_all(lax.all_to_all(candidates, 'pb', split_axis=0, concat_axis...  9.97 us
    top_k x1, other arithmetic, local(): leaders, _ = lax.top_k(pooled, K)  8.39 us
    unnamed x10, local copies, waits for them, and re-layouts  7.93 us
    all_to_all x1, blocking collectives, local(): lax.all_to_all(candidates, 'pb', split_axis=0, concat_axis=1, tiled=True)  6.3 us

commit v1 on v0

--- a/solution.py
+++ b/solution.py
@@ -7,6 +7,29 @@
 K = 100
 NLIST = 1024
 masked_value = -1e30
+
+
+def split_up(shard, dim, devices):
+    shape = shard.shape
+    blocks = shard.reshape(*shape[:dim], devices, shape[dim] // devices, *shape[dim + 1 :])
+    return jnp.moveaxis(blocks, dim, 0)
+
+
+def laid_out(pieces, dim):
+    pieces = jnp.moveaxis(pieces, 0, dim)
+    lengths = pieces.shape
+    return pieces.reshape(*lengths[:dim], lengths[dim] * lengths[dim + 1], *lengths[dim + 2 :])
+
+
+def pairwise_exchange(value, axis, split_dim, concat_dim):
+    count, index = (lax.axis_size(axis), lax.axis_index(axis))
+    pieces = split_up(value, split_dim, count)
+    outs = [pieces[index]]
+    for step in range(1, count):
+        sent = pieces[index ^ step]
+        outs.append(lax.ppermute(sent, axis, [(i, i ^ step) for i in range(count)]))
+    pieces = jnp.stack(outs)[index ^ jnp.arange(count)]
+    return laid_out(pieces, concat_dim)
 
 
 def filtered_scores(block_rows, block_probes, slab_part, list_onehot):
@@ -47,12 +70,8 @@
         ),
     )
     candidates = kept.reshape(count, local_count)
-    pooled = lax.all_to_all(
-        lax.all_to_all(candidates, "pb", split_axis=0, concat_axis=1, tiled=True),
-        "dev",
-        split_axis=0,
-        concat_axis=1,
-        tiled=True,
+    pooled = pairwise_exchange(
+        lax.all_to_all(candidates, "pb", split_axis=0, concat_axis=1, tiled=True), "dev", 0, 1
     )
     leaders, _ = lax.top_k(pooled, K)
     return leaders

time: 174 us -> 180 us (1.034)
  blocking collectives: 151 us -> 134 us
  starting transfers between devices: 0 us -> 14.9 us
  waiting for transfers between devices: 0 us -> 6.65 us
    all_to_all x2 -> x0, blocking collectives: 16.3 us -> none  [the longest x1 9.97 us: local(): lax.all_to_all(lax.all_to_all(candidates, 'pb', split_axis=0, concat_axis...]
    ppermute x0 -> x7, starting transfers between devices: none -> 11.5 us  [pairwise_exchange(): outs.append(lax.ppermute(sent, axis, [(i, i ^ step) for i in range(count)]))]
    all_to_all x0 -> x1, waiting for transfers between devices: none -> 3.67 us  [local(): lax.all_to_all(candidates, 'pb', split_axis=0, concat_axis=1, tiled=True)]
    all_to_all x0 -> x1, starting transfers between devices: none -> 3.44 us  [local(): lax.all_to_all(candidates, 'pb', split_axis=0, concat_axis=1, tiled=True)]
    ppermute x0 -> x7, waiting for transfers between devices: none -> 2.98 us  [pairwise_exchange(): outs.append(lax.ppermute(sent, axis, [(i, i ^ step) for i in range(count)]))]
    unnamed x10 -> x16, local copies, waits for them, and re-layouts: 7.93 us -> 7.98 us
  transfers between devices with their start and end apart: 0 -> 8, of which waited for: 0 -> 3; matrix products, arithmetic and copies ran while one was open for 0% -> 0% of each run, Pallas kernels for 0% -> 0%
where the time goes in v1:
time: 180 us
  blocking collectives  134 us (74%)
  starting transfers between devices  14.9 us (8%)
  other arithmetic  13.7 us (8%)
  local copies, waits for them, and re-layouts  9.47 us (5%)
  waiting for transfers between devices  6.65 us (4%)
    all_gather x2, blocking collectives, local(): lax.all_gather((queries, probes), ('pb', 'dev'), axis=0, tiled=True)  134 us
    ppermute x7, starting transfers between devices, pairwise_exchange(): outs.append(lax.ppermute(sent, axis, [(i, i ^ step) for i in range(count)]))  11.5 us
    top_k x1, other arithmetic, local(): leaders, _ = lax.top_k(pooled, K)  8.39 us
    unnamed x16, local copies, waits for them, and re-layouts  7.98 us
    top_k x1, other arithmetic, one_block(): lax.top_k(filtered_scores(rows_here, probes_here, vectors, list_onehot),...  3.79 us
    all_to_all x1, waiting for transfers between devices, local(): lax.all_to_all(candidates, 'pb', split_axis=0, concat_axis=1, tiled=True)  3.67 us
  transfers between devices with their start and end apart: 8, of which 3 were waited for; matrix products, arithmetic and copies ran while one was open for 0% of the time, Pallas kernels for 0%

profile of v1, /device:TPU:0, one launch (start us, length us, event | category | flops | bytes accessed | tf_op | source)
XLA Modules:
  0.0 180.0 jit_solution(927660027667059949)
XLA Ops:
  0.0 70.2 %all-gather = s32[32,2,16]{2,1,0:T(2,128)S(1)} all-gather(s32[1,2,16]{2,1,0:T(2,128)} %bitcast.45), channel_id=1, replica_groups=mesh['pb'=4,'dev'=8] {'pb','dev'}, dimensions={0}, use_global_device_ids=true | all-gather | bytes 4224 | tf_op jit(solution)/shard_map/all_gather | solution.py:54
  70.2 0.1 copy.13
  70.3 0.7 and_reduce_fusion
  71.0 0.7 multiply_reduce_fusion
  71.8 0.1 copy.16
  71.8 0.1 reshape.61
  71.9 7.7 %scatter_custom_fusion = bf16[65536]{0:T(1024)(128)(2,1)S(1)} fusion(s32[1024]{0:T(1024)S(1)} %reshape.61, bf16[1024]{0:T(1024)(128)(2,1)S(1)} %broadcast.93, bf16[]{:T(256)} %constant.54.clone.1), kind=kCustom, calls=%fused_computation.7 | custom fusion | bytes 131074
  79.6 0.1 reshape.52
  79.7 64.1 %all-gather.1 = bf16[32,2,768]{2,1,0:T(2,128)(2,1)S(1)} all-gather(bf16[1,2,768]{2,1,0:T(2,128)(2,1)} %bitcast.44), channel_id=1, replica_groups=mesh['pb'=4,'dev'=8] {'pb','dev'}, dimensions={0}, use_global_device_ids=true | all-gather | bytes 101376 | tf_op jit(solution)/shard_map/all_gather | solution.py:54
  143.8 0.5 fusion.1
  144.3 0.4 convolution_select_fusion
  144.7 3.8 %sort_prefixfusion = f32[64,100]{1,0:T(8,128)} fusion(f32[64,512]{1,0:T(8,128)S(1)} %convolution_select_fusion), kind=kCustom, calls=%top_k.14.sort_prefix | custom fusion | flops 491520 | bytes 156672 | tf_op jit(solution)/shard_map/while/body/eval_jaxpr/top_k | solution.py:60
  148.5 3.4 %all-to-all-start = ((f32[4,16,100]{2,1,0:T(8,128)}), f32[4,16,100]{2,1,0:T(8,128)S(1)}, u32[]{:S(2)}, u32[]{:S(2)}) async-start(f32[4,16,100]{2,1,0:T(8,128)} %bitcast.4), calls=%async_computation | async-start | bytes 65536 | tf_op jit(solution)/shard_map/all_to_all | solution.py:74
  152.0 3.7 %all-to-all-done = f32[4,16,100]{2,1,0:T(8,128)S(1)} async-done(((f32[4,16,100]{2,1,0:T(8,128)}), f32[4,16,100]{2,1,0:T(8,128)S(1)}, u32[]{:S(2)}, u32[]{:S(2)}) %all-to-all-start) | async-done | bytes 25632 | tf_op jit(solution)/shard_map/all_to_all | solution.py:74
  155.7 0.1 reshape.47
  155.8 2.3 %collective-permute-start = (f32[2,400]{1,0:T(2,128)S(1)}, f32[2,400]{1,0:T(2,128)S(1)}, u32[]{:S(2)}, u32[]{:S(2)}) collective-permute-start(f32[2,400]{1,0:T(2,128)S(1)} %get-tuple-element.36), channel_id=1, source_target_pairs={{0,1},{1,0},{2,3},{3,2},{4,5},{5,4},{6,7},{7,6},{8,9},{9,8},{10,11... | collective-permute-start | bytes 9608 | tf_op jit(solution)/shard_map/ppermute | solution.py:30
  158.1 0.0 collective-permute-start.1
  158.1 1.5 collective-permute-start.2
  159.7 0.0 collective-permute-start.3
  159.7 4.3 %collective-permute-start.4 = (f32[2,400]{1,0:T(2,128)S(1)}, f32[2,400]{1,0:T(2,128)S(1)}, u32[]{:S(2)}, u32[]{:S(2)}) collective-permute-start(f32[2,400]{1,0:T(2,128)S(1)} %get-tuple-element.32), channel_id=1, source_target_pairs={{0,5},{1,4},{2,7},{3,6},{4,1},{5,0},{6,3},{7,2},{8,13},{9,12},{10,... | collective-permute-start | bytes 9608 | tf_op jit(solution)/shard_map/ppermute | solution.py:30
  164.0 0.0 collective-permute-done
  164.0 0.0 collective-permute-start.5
  164.0 3.3 %collective-permute-start.6 = (f32[2,400]{1,0:T(2,128)S(1)}, f32[2,400]{1,0:T(2,128)S(1)}, u32[]{:S(2)}, u32[]{:S(2)}) collective-permute-start(f32[2,400]{1,0:T(2,128)S(1)} %get-tuple-element.30), channel_id=1, source_target_pairs={{0,7},{1,6},{2,5},{3,4},{4,3},{5,2},{6,1},{7,0},{8,15},{9,14},{10,... | collective-permute-start | bytes 9608 | tf_op jit(solution)/shard_map/ppermute | solution.py:30
  167.3 0.0 collective-permute-done.2
  167.3 0.0 collective-permute-done.3
  167.4 0.0 collective-permute-done.4
  167.4 2.0 %collective-permute-done.5 = f32[2,400]{1,0:T(2,128)S(1)} collective-permute-done((f32[2,400]{1,0:T(2,128)S(1)}, f32[2,400]{1,0:T(2,128)S(1)}, u32[]{:S(2)}, u32[]{:S(2)}) %collective-permute-start.5) | collective-permute-done | bytes 3232 | tf_op jit(solution)/shard_map/ppermute | solution.py:30
  169.4 1.0 collective-permute-done.6
  170.4 0.6 gather_fusion
  171.0 0.1 reshape.48
  171.1 8.4 %top_k.20 = (f32[2,3200]{1,0:T(2,128)S(1)}, s32[2,3200]{1,0:T(2,128)}) sort(f32[2,3200]{1,0:T(2,128)S(1)} %reshape.48, s32[2,3200]{1,0:T(2,128)S(1)} %iota.29), dimensions={1}, to_apply=%region_2.3 | sort | flops 83200 | bytes 102400 | tf_op jit(solution)/shard_map/top_k | solution.py:76
  179.5 0.6 top_k.21
  (23 shorter events, 0.2 us)
Async XLA Ops:
  0.0 144.3 %copy-start = (bf16[512,768]{1,0:T(8,128)(2,1)S(1)}, bf16[512,768]{1,0:T(8,128)(2,1)}, u32[]{:S(2)}) copy-start(bf16[512,768]{1,0:T(8,128)(2,1)} %param.6) | copy-start | bytes 2359300
  0.0 143.8 %copy-start.1 = (s32[512]{0:T(512)S(1)}, s32[512]{0:T(512)}, u32[]{:S(2)}) copy-start(s32[512]{0:T(512)} %param.7) | copy-start | bytes 6148
  148.5 7.2 %all-to-all-start = ((f32[4,16,100]{2,1,0:T(8,128)}), f32[4,16,100]{2,1,0:T(8,128)S(1)}, u32[]{:S(2)}, u32[]{:S(2)}) async-start(f32[4,16,100]{2,1,0:T(8,128)} %bitcast.4), calls=%async_computation | async-start | bytes 65536 | tf_op jit(solution)/shard_map/all_to_all | solution.py:74
  155.8 8.1 %collective-permute-start = (f32[2,400]{1,0:T(2,128)S(1)}, f32[2,400]{1,0:T(2,128)S(1)}, u32[]{:S(2)}, u32[]{:S(2)}) collective-permute-start(f32[2,400]{1,0:T(2,128)S(1)} %get-tuple-element.36), channel_id=1, source_target_pairs={{0,1},{1,0},{2,3},{3,2},{4,5},{5,4},{6,7},{7,6},{8,9},{9,8},{10,11... | collective-permute-start | bytes 9608 | tf_op jit(solution)/shard_map/ppermute | solution.py:30
  158.1 5.9 %collective-permute-start.1 = (f32[2,400]{1,0:T(2,128)S(1)}, f32[2,400]{1,0:T(2,128)S(1)}, u32[]{:S(2)}, u32[]{:S(2)}) collective-permute-start(f32[2,400]{1,0:T(2,128)S(1)} %get-tuple-element.35), channel_id=1, source_target_pairs={{0,2},{1,3},{2,0},{3,1},{4,6},{5,7},{6,4},{7,5},{8,10},{9,11},{10,... | collective-permute-start | bytes 9608 | tf_op jit(solution)/shard_map/ppermute | solution.py:30
  158.1 9.2 %collective-permute-start.2 = (f32[2,400]{1,0:T(2,128)S(1)}, f32[2,400]{1,0:T(2,128)S(1)}, u32[]{:S(2)}, u32[]{:S(2)}) collective-permute-start(f32[2,400]{1,0:T(2,128)S(1)} %get-tuple-element.34), channel_id=1, source_target_pairs={{0,3},{1,2},{2,1},{3,0},{4,7},{5,6},{6,5},{7,4},{8,11},{9,10},{10,... | collective-permute-start | bytes 9608 | tf_op jit(solution)/shard_map/ppermute | solution.py:30
  159.7 7.7 %collective-permute-start.3 = (f32[2,400]{1,0:T(2,128)S(1)}, f32[2,400]{1,0:T(2,128)S(1)}, u32[]{:S(2)}, u32[]{:S(2)}) collective-permute-start(f32[2,400]{1,0:T(2,128)S(1)} %get-tuple-element.33), channel_id=1, source_target_pairs={{0,4},{1,5},{2,6},{3,7},{4,0},{5,1},{6,2},{7,3},{8,12},{9,13},{10,... | collective-permute-start | bytes 9608 | tf_op jit(solution)/shard_map/ppermute | solution.py:30
  159.7 7.7 %collective-permute-start.4 = (f32[2,400]{1,0:T(2,128)S(1)}, f32[2,400]{1,0:T(2,128)S(1)}, u32[]{:S(2)}, u32[]{:S(2)}) collective-permute-start(f32[2,400]{1,0:T(2,128)S(1)} %get-tuple-element.32), channel_id=1, source_target_pairs={{0,5},{1,4},{2,7},{3,6},{4,1},{5,0},{6,3},{7,2},{8,13},{9,12},{10,... | collective-permute-start | bytes 9608 | tf_op jit(solution)/shard_map/ppermute | solution.py:30
  164.0 5.4 %collective-permute-start.5 = (f32[2,400]{1,0:T(2,128)S(1)}, f32[2,400]{1,0:T(2,128)S(1)}, u32[]{:S(2)}, u32[]{:S(2)}) collective-permute-start(f32[2,400]{1,0:T(2,128)S(1)} %get-tuple-element.31), channel_id=1, source_target_pairs={{0,6},{1,7},{2,4},{3,5},{4,2},{5,3},{6,0},{7,1},{8,14},{9,15},{10,... | collective-permute-start | bytes 9608 | tf_op jit(solution)/shard_map/ppermute | solution.py:30
  164.0 6.4 %collective-permute-start.6 = (f32[2,400]{1,0:T(2,128)S(1)}, f32[2,400]{1,0:T(2,128)S(1)}, u32[]{:S(2)}, u32[]{:S(2)}) collective-permute-start(f32[2,400]{1,0:T(2,128)S(1)} %get-tuple-element.30), channel_id=1, source_target_pairs={{0,7},{1,6},{2,5},{3,4},{4,3},{5,2},{6,1},{7,0},{8,15},{9,14},{10,... | collective-permute-start | bytes 9608 | tf_op jit(solution)/shard_map/ppermute | solution.py:30
